TPU v7x, 128 devices: a whole 4x4x4 slice. The times are simulated.
128 devices in a mesh: gx: 16 (over y, z), gy: 8 (over x, core).
Axes of the slice: x: 4, y: 4, z: 4, core: 2. Of those that a mesh axis runs over, the one named last changes fastest.
Arguments:
- state: float32 [4, 5, 5, 128, 2048], P(None, None, None, 'gy', 'gx'), may hold values from -3 to 60, as said below
Outputs:
- advanced: float32 [4, 5, 5, 128, 2048], P(None, None, None, 'gy', 'gx')
- tendency: float32 [4, 5, 5, 128, 2048], P(None, None, None, 'gy', 'gx')
Inputs may be any that keep to these rules, and one draw needn't show every extreme that they name: `state`: at every node density is at least 0.2 and pressure, 0.4 times (energy minus half the squared momentum over density), is at least 0.2.
All inputs are finite; a program needn't handle non-finite values.
Results may differ from a plain program's by a relative error of at most 0.0003.
Values sent between devices are 32-bit elements; how exact they have to be, the bound alone decides.
No kernel may reach another device: no remote copies, remote signals or barrier semaphores. Data moves between devices by JAX's collectives and lax.ppermute only.
A program may use at most 128 MiB of HBM per device.

v0:
```python
import math

import jax
import jax.numpy as jnp
import numpy as np
from jax import lax
from jax.experimental import pallas as pl
from jax.experimental.pallas import tpu as pltpu
from jax.sharding import Mesh
from jax.sharding import PartitionSpec as P


GX = ("gx_0", "gx_1")
GY = ("gy_0", "gy_1")
ALL = ("gx_0", "gx_1", "gy_0", "gy_1")


ADIABATIC = 1.4
COURANT = 0.2
ALPHA_MAX = 0.5
ROWS = 16
COLS = 128
F32 = jnp.float32


def tables():
    lobatto = np.array([-1.0, -math.sqrt(3.0 / 7.0), 0.0, math.sqrt(3.0 / 7.0), 1.0])
    weights = np.array([0.1, 49.0 / 90.0, 32.0 / 45.0, 49.0 / 90.0, 0.1])
    identity = np.eye(5)
    distance = lobatto[:, None] - lobatto[None, :] + identity
    barycentric = 1.0 / np.prod(distance, axis=1)
    derivative = (1.0 - identity) * (barycentric[None, :] / barycentric[:, None]) / distance
    derivative = derivative - identity * derivative.sum(axis=1)[:, None]
    legendre = np.zeros((5, 5))
    legendre[:, 0] = 1.0
    legendre[:, 1] = lobatto
    for degree in range(2, 5):
        legendre[:, degree] = (
            (2 * degree - 1) * lobatto * legendre[:, degree - 1]
            - (degree - 1) * legendre[:, degree - 2]
        ) / degree
    norms = np.array([2.0, 2.0 / 3.0, 2.0 / 5.0, 2.0 / 7.0, 0.5])
    inverse = (legendre * weights[:, None]).T / norms[:, None]
    return derivative, weights, inverse


DERIVATIVE, WEIGHTS, INVERSE = tables()
SKEW = WEIGHTS[:, None] * DERIVATIVE
PER_WEIGHT = 1.0 / WEIGHTS
SCALE = (1.0, 0.5, 0.5, 0.5)
LN2 = math.log(2.0)


LN2 = math.log(2.0)
NEAR = math.log2(1.01 / 0.99)


def velocity_pressure(rho, mx, my, en):
    inv_rho = 1.0 / rho
    vx = mx * inv_rho
    vy = my * inv_rho
    pressure = 0.4 * en - 0.2 * (mx * vx + my * vy)
    return vx, vy, pressure, inv_rho


def sound(theta):
    square = (ADIABATIC / (5.0 * LN2)) * theta
    return square * lax.rsqrt(square)


def derived(rho, mx, my, en):
    vx, vy, p, inv_rho = velocity_pressure(rho, mx, my, en)
    theta = (5.0 * LN2) * (p * inv_rho)
    return vx, vy, p, rho * ((0.2 / LN2) / p), theta, inv_rho, sound(theta)


class Node:
    def __init__(self, cons, values, normal):
        rho, mx, my, en = cons
        vx, vy, p, beta, theta, inv_rho, c = values
        self.rho, self.en, self.p = rho, en, p
        self.beta, self.theta, self.inv_rho = beta, theta, inv_rho
        self.vn, self.vt, self.mn, self.mt = (vx, vy, mx, my) if normal == 0 else (vy, vx, my, mx)
        self.speed = jnp.abs(self.vn) + c
        self.cons = (rho, self.mn, self.mt, en)


def series(f):
    c = [2.0 / (k * LN2) for k in (1, 3, 5, 7)]
    return c[0] + f * (c[1] + f * (c[2] + f * c[3]))


def pair(left, right, q):
    s = left.rho + right.rho
    d = right.rho - left.rho
    logged = lax.log2(right.rho * left.inv_rho)
    near = jnp.abs(logged) < NEAR
    t = d * (1.0 / jnp.where(near, s, logged))
    mean = jnp.where(near, s * (1.0 / series(t * t)), t)
    s = left.beta + right.beta
    d = right.beta - left.beta
    logged = lax.log2(right.beta * left.theta)
    near = jnp.abs(logged) < NEAR
    r = 1.0 / jnp.where(near, s, d)
    t = d * r
    warm = jnp.where(near, series(t * t), logged) * r
    vn = left.vn + right.vn
    vt = left.vt + right.vt
    ps = left.p + right.p
    cross = left.p * right.vn + right.p * left.vn
    if q != 0.5:
        ps = ps * (2.0 * q)
        cross = cross * (2.0 * q)
    mass = (mean * vn) * (q / LN2)
    along = mass * vn + ps
    across = mass * vt
    dot = left.vn * right.vn + left.vt * right.vt
    energy = mass * (dot + warm) + cross
    return mass, along, across, energy


def line_terms(nodes, lower, upper):
    high = [[None] * 5 for _ in range(4)]
    for j in range(4, 0, -1):
        for i in range(j):
            flux = pair(nodes[i], nodes[j], float(SKEW[i, j]))
            for v in range(4):
                high[v][i] = flux[v] if high[v][i] is None else high[v][i] + flux[v]
                if j == 4:
                    high[v][4] = flux[v] if high[v][4] is None else high[v][4] + flux[v]
                else:
                    high[v][j] = high[v][j] - flux[v]
    own = []
    for node in nodes:
        flow = node.mn * node.vn + node.p
        own.append((node.mn, flow, node.mn * node.vt, node.vn * (node.en + node.p)))
    low = [[None] * 5 for _ in range(4)]
    for v in range(4):
        before = None
        for i in range(4):
            spread = jnp.maximum(nodes[i].speed, nodes[i + 1].speed)
            jump = nodes[i + 1].cons[v] - nodes[i].cons[v]
            inner = own[i][v] + own[i + 1][v] - spread * jump
            low[v][i] = inner if before is None else inner - before
            before = inner
        low[v][4] = before
        for i, flux in ((0, lower[v]), (4, upper[v])):
            high[v][i] = high[v][i] - flux
            low[v][i] = low[v][i] - (flux + flux if v == 0 else flux)
    return high, low


def face(left, right):
    flux = pair(left, right, 0.5)
    fastest = jnp.maximum(left.speed, right.speed)
    out = []
    for v in range(4):
        jump = fastest * (right.cons[v] - left.cons[v])
        out.append(flux[v] - (0.5 * jump if v == 0 else jump))
    return out


def transform(values):
    s0, s1 = values[0] + values[4], values[1] + values[3]
    d0, d1 = values[0] - values[4], values[1] - values[3]
    out = []
    for k in range(5):
        c = [float(x) for x in INVERSE[k]]
        if k % 2 == 0:
            out.append(c[0] * s0 + c[1] * s1 + c[2] * values[2])
        else:
            out.append(c[0] * d0 + c[1] * d1)
    return out


def raw_indicator(indicator):
    along = [transform(indicator[a]) for a in range(5)]
    modal = [transform([along[a][l] for a in range(5)]) for l in range(5)]
    levels = [None] * 5
    for l in range(5):
        for k in range(5):
            square = modal[l][k] * modal[l][k]
            level = max(k, l)
            levels[level] = square if levels[level] is None else levels[level] + square
    lower = levels[0] + levels[1] + levels[2] + levels[3]
    total = lower + levels[4]
    energy = jnp.maximum(levels[4] / total, levels[3] / lower)
    threshold = 0.5 * 10.0 ** (-1.8 * 5.0**0.25)
    sharpness = math.log((1.0 - 0.0001) / 0.0001)
    sigmoid = 1.0 / (1.0 + jnp.exp(-sharpness / threshold * (energy - threshold)))
    return jnp.minimum(sigmoid, ALPHA_MAX)


def lanes():
    return lax.broadcasted_iota(jnp.int32, (8, COLS), 1)


def sublanes():
    return lax.broadcasted_iota(jnp.int32, (8, COLS), 0)


def odd_column():
    return lax.rem(lax.axis_index("gx_1"), 2)


def odd_row():
    return lax.axis_index("gy_1")


def pack_borders(get, raws, cols_ref, even_ref, odd_ref, both_ref):
    up_ref, down_ref = both_ref.at[0], both_ref.at[1]
    lane = lanes()
    for i in range(2):
        packed = jnp.zeros((8, COLS), F32)
        for v in range(4):
            for a in range(5):
                j = v * 5 + a
                first = get(v, a, 0, pl.ds(8 * i, 8))
                last = get(v, a, 4, pl.ds(8 * i, 8))
                packed = jnp.where(lane == j, first if j == 0 else pltpu.roll(first, j, 1), packed)
                packed = jnp.where(lane == 64 + j, pltpu.roll(last, 65 + j, 1), packed)
        packed = jnp.where(lane == 20, pltpu.roll(raws[i], 20, 1), packed)
        packed = jnp.where(lane == 84, pltpu.roll(raws[i], 85, 1), packed)
        cols_ref[pl.ds(8 * i, 8), :] = packed
    for v in range(4):
        for b in range(5):
            j = v * 5 + b
            up_ref[j : j + 1, :] = get(v, 4, b, pl.ds(15, 1))
            down_ref[j : j + 1, :] = get(v, 0, b, pl.ds(0, 1))
    up_ref[20:21, :] = raws[1][7:8, :]
    down_ref[20:21, :] = raws[0][0:1, :]
    zeros = jnp.zeros((3, COLS), F32)
    up_ref[21:24, :] = zeros
    down_ref[21:24, :] = zeros
    odd = odd_row()
    even_ref[...] = both_ref[odd]
    odd_ref[...] = both_ref[1 - odd]


def unpack_borders(col_even_ref, col_odd_ref, row_even_ref, row_odd_ref, cols_ref, rows_ref):
    cols_ref[0] = col_even_ref[...]
    cols_ref[1] = col_odd_ref[...]
    rows_ref[0] = row_even_ref[...]
    rows_ref[1] = row_odd_ref[...]
    odd = odd_column()
    left, right = cols_ref.at[1 - odd], cols_ref.at[odd]
    odd = odd_row()
    below, above = rows_ref.at[1 - odd], rows_ref.at[odd]
    return left, right, below, above


def own_borders(cols_ref, even_ref, odd_ref, rows_ref):
    rows_ref[0] = even_ref[...]
    rows_ref[1] = odd_ref[...]
    odd = odd_row()
    return cols_ref, (rows_ref.at[1 - odd], rows_ref.at[odd])


def start_kernel(state_ref, top_ref, u_ref, arrived):
    copies = [
        pltpu.make_async_copy(state_ref.at[:, a], u_ref.at[:, a], arrived.at[a]) for a in range(5)
    ]
    for copy in copies:
        copy.start()
    tops = [None, None]
    for a in range(5):
        copies[a].wait()
        for i in range(2):
            rows = pl.ds(8 * i, 8)
            for b in range(5):
                rho, mx, my, en = (u_ref[v, a, b, rows, :] for v in range(4))
                vx, vy, p, inv_rho = velocity_pressure(rho, mx, my, en)
                square = vx * vx + vy * vy
                speed = square * lax.rsqrt(jnp.maximum(square, 1e-37))
                square = ADIABATIC * (p * inv_rho)
                speed = speed + square * lax.rsqrt(square)
                tops[i] = speed if tops[i] is None else jnp.maximum(tops[i], speed)
    top = jnp.max(jnp.maximum(tops[0], tops[1]), axis=0, keepdims=True)
    top_ref[...] = jnp.broadcast_to(top.reshape(1, 1, COLS), top_ref.shape)


def border_kernel(u_ref, raw_ref, cols_ref, even_ref, odd_ref, both_ref):
    raws = []
    for i in range(2):
        rows = pl.ds(8 * i, 8)
        indicator = [[None] * 5 for _ in range(5)]
        for a in range(5):
            for b in range(5):
                cons = [u_ref[v, a, b, rows, :] for v in range(4)]
                indicator[a][b] = cons[0] * velocity_pressure(*cons)[2]
        raws.append(raw_indicator(indicator))
        raw_ref[rows, :] = raws[i]
    pack_borders(
        lambda v, a, b, rows: u_ref[v, a, b, rows, :], raws, cols_ref, even_ref, odd_ref, both_ref
    )


ORDER = ((0, 1, 2, 3), (0, 2, 1, 3))


def node_at(u_ref, work_ref, a, b, normal, load):
    cons = [load(u_ref, (v, a, b)) for v in range(4)]
    return Node(cons, [load(work_ref, (k, a, b)) for k in range(7)], normal)


def row_faces(u_ref, work_ref, faces_ref):
    sublane = sublanes()
    for b in range(5):
        fluxes = []
        for i in range(2):
            rows = pl.ds(8 * i, 8)

            def above(ref, index, i=i):
                if i == 0:
                    return ref[(*index, pl.ds(1, 8), slice(None))]
                return pltpu.roll(ref[(*index, pl.ds(8, 8), slice(None))], 7, 0)

            def here(ref, index, rows=rows):
                return ref[(*index, rows, slice(None))]

            left = node_at(u_ref, work_ref, 4, b, 1, here)
            right = node_at(u_ref, work_ref, 0, b, 1, above)
            fluxes.append(face(left, right))
        for v in range(4):
            first = fluxes[0][v]
            second = jnp.where(sublane == 7, 0.0, fluxes[1][v])
            rolled = pltpu.roll(first, 1, 0)
            faces_ref[0, v, b, 0:8, :] = jnp.where(sublane == 0, 0.0, rolled)
            faces_ref[0, v, b, 8:16, :] = jnp.where(sublane == 0, rolled, pltpu.roll(second, 1, 0))
            faces_ref[1, v, b, 0:8, :] = first
            faces_ref[1, v, b, 8:16, :] = second


def volume_kernel(u_ref, work_ref, high_ref, low_ref, faces_ref):
    row_faces(u_ref, work_ref, faces_ref)
    lane = lanes()

    def chunk(i, carry):
        rows = pl.ds(pl.multiple_of(8 * i, 8), 8)

        def here(ref, index):
            return ref[(*index, rows, slice(None))]

        def after(ref, index):
            return pltpu.roll(here(ref, index), 127, 1)

        for normal in range(2):
            for across in range(5):
                places = [(across, k) if normal == 0 else (k, across) for k in range(5)]
                nodes = [node_at(u_ref, work_ref, a, b, normal, here) for a, b in places]
                if normal == 0:
                    flux = face(nodes[4], node_at(u_ref, work_ref, across, 0, 0, after))
                    upper = [jnp.where(lane == 127, 0.0, x) for x in flux]
                    lower = [pltpu.roll(x, 1, 1) for x in upper]
                else:
                    lower, upper = (
                        [faces_ref[k, v, across, rows, :] for v in range(4)] for k in range(2)
                    )
                sums = line_terms(nodes, lower, upper)
                for ref, terms in zip((high_ref, low_ref), sums):
                    for along, (a, b) in enumerate(places):
                        for k in range(4):
                            v = ORDER[normal][k]
                            term = terms[k][along]
                            if normal == 1:
                                ratio = float(WEIGHTS[b] / WEIGHTS[a])
                                if a not in (b, 4 - b):
                                    term = ratio * term
                                before = ref[v, a, b, rows, :]
                                term = before - term if (a == 4) != (b == 4) else before + term
                            ref[v, a, b, rows, :] = term
        return carry

    lax.fori_loop(0, 2, chunk, 0)


def first_volume_kernel(u_ref, high_ref, low_ref, work_ref, faces_ref):
    def chunk(i, carry):
        rows = pl.ds(pl.multiple_of(8 * i, 8), 8)
        for a in range(5):
            for b in range(5):
                for k, x in enumerate(derived(*(u_ref[v, a, b, rows, :] for v in range(4)))):
                    work_ref[k, a, b, rows, :] = x
        return carry

    lax.fori_loop(0, 2, chunk, 0)
    volume_kernel(u_ref, work_ref, high_ref, low_ref, faces_ref)


def plain(cons, normal):
    return Node(cons, derived(*cons), normal)


def rates(i, high_ref, low_ref, raw_ref, mine, halos, edge_ref):
    my_cols_ref, my_rows_ref = mine
    left_ref, right_ref, below_ref, above_ref = halos
    rows = pl.ds(8 * i, 8)
    lane, sublane = lanes(), sublanes()
    from_left, from_right, own = left_ref[rows, :], right_ref[rows, :], my_cols_ref[rows, :]

    capped = raw_ref[rows, :]
    row_before = below_ref[20:21, :] if i == 0 else raw_ref[7:8, :]
    row_after = above_ref[20:21, :] if i == 1 else raw_ref[8:9, :]
    below = jnp.where(sublane == 0, jnp.broadcast_to(row_before, (8, COLS)), pltpu.roll(capped, 1, 0))
    above = jnp.where(sublane == 7, jnp.broadcast_to(row_after, (8, COLS)), pltpu.roll(capped, 7, 0))
    before = jnp.where(lane == 0, pltpu.roll(from_left, 44, 1), pltpu.roll(capped, 1, 1))
    after = jnp.where(lane == 127, pltpu.roll(from_right, 107, 1), pltpu.roll(capped, 127, 1))
    beside = jnp.maximum(jnp.maximum(below, above), jnp.maximum(before, after))
    blend = jnp.maximum(capped, 0.5 * beside)
    rest = 1.0 - blend
    shares = (0.5 * blend, blend, blend, blend)

    lefts, rights = [], []
    for v in range(4):
        shifted = own if v == 0 else pltpu.roll(own, COLS - 5 * v, 1)
        lefts.append(jnp.where(lane < 64, pltpu.roll(from_left, 64 - 5 * v, 1), shifted))
        rights.append(jnp.where(lane < 64, shifted, pltpu.roll(from_right, 64 - 5 * v, 1)))
    used = jnp.bitwise_and(lane, 63) < 5
    filler = (1.0, 0.0, 0.0, 1.0)
    lefts = [jnp.where(used, x, y) for x, y in zip(lefts, filler)]
    rights = [jnp.where(used, x, y) for x, y in zip(rights, filler)]
    ends = {}
    flux = face(plain(lefts, 0), plain(rights, 0))
    for v in range(4):
        for a in range(5):
            turned = flux[v] if a == 0 else pltpu.roll(flux[v], COLS - a, 1)
            ends[v, a, 0] = jnp.where(lane == 0, turned, 0.0)
            ends[v, a, 4] = jnp.where(lane == 127, pltpu.roll(flux[v], 63 - a, 1), 0.0)
    a = 4 * i
    other_ref = (below_ref, above_ref)[i]
    mine_at = my_rows_ref[i]
    other = [other_ref[5 * v : 5 * v + 5, :] for v in range(4)]
    here = [mine_at[5 * v : 5 * v + 5, :] for v in range(4)]
    sides = (plain(other, 1), plain(here, 1)) if i == 0 else (plain(here, 1), plain(other, 1))
    flux = face(*sides)
    edge = sublane == 7 * i
    for k in range(4):
        v = ORDER[1][k]
        edge_ref[i, 8 * v : 8 * v + 5, :] = flux[k]
        for b in range(5):
            term = jnp.broadcast_to(edge_ref[i, 8 * v + b : 8 * v + b + 1, :], (8, COLS))
            if b not in (0, 4):
                term = float(WEIGHTS[b] / WEIGHTS[a]) * term
            term = jnp.where(edge, term, 0.0)
            same = (a == 4) == (b == 4)
            if (v, a, b) in ends:
                ends[v, a, b] = ends[v, a, b] + term if same else ends[v, a, b] - term
            else:
                ends[v, a, b] = term if a == 0 else -term

    def at(v, a, b):
        x = rest * high_ref[v, a, b, rows, :] + shares[v] * low_ref[v, a, b, rows, :]
        return x - ends[v, a, b] if (v, a, b) in ends else x

    return at


NODES = [(a, b, v) for a in range(5) for b in range(5) for v in range(4)]


def final(v, b):
    return (1.0 if b == 4 else -1.0) * float(PER_WEIGHT[b]) * SCALE[v]


def step_of(tops_ref):
    tops = [tops_ref[k] for k in range(128)]
    while len(tops) > 1:
        tops = [jnp.maximum(x, y) for x, y in zip(tops[::2], tops[1::2])]
    top = jnp.max(tops[0], axis=1, keepdims=True)
    return (COURANT * 2.0 / 9.0) / jnp.broadcast_to(top, (8, COLS))


def first_kernel(
    tops_ref, u_ref, high_ref, low_ref, raw_ref, my_cols_ref, my_even_ref, my_odd_ref, col_even_ref, col_odd_ref, row_even_ref, row_odd_ref,
    step_ref, first_ref, next_raw_ref, next_work_ref, cols_ref, even_ref, odd_ref, both_ref, got_cols_ref, got_rows_ref, my_rows_ref, edge_ref,
):
    step = step_of(tops_ref)
    step_ref[...] = step
    steps = {(v, b): final(v, b) * step for v in (0, 1) for b in range(5)}
    halos = unpack_borders(
        col_even_ref, col_odd_ref, row_even_ref, row_odd_ref, got_cols_ref, got_rows_ref
    )

    mine = own_borders(my_cols_ref, my_even_ref, my_odd_ref, my_rows_ref)

    raws = []
    for i in range(2):
        rows = pl.ds(8 * i, 8)
        at = rates(i, high_ref, low_ref, raw_ref, mine, halos, edge_ref)
        for a, b, v in NODES:
            first_ref[v, a, b, rows, :] = u_ref[v, a, b, rows, :] + steps[min(v, 1), b] * at(v, a, b)
        indicator = [[None] * 5 for _ in range(5)]
        for a in range(5):
            for b in range(5):
                cons = [first_ref[v, a, b, rows, :] for v in range(4)]
                values = derived(*cons)
                for k, x in enumerate(values):
                    next_work_ref[k, a, b, rows, :] = x
                indicator[a][b] = cons[0] * values[2]
        raws.append(raw_indicator(indicator))
        next_raw_ref[rows, :] = raws[i]
    pack_borders(
        lambda v, a, b, rows: first_ref[v, a, b, rows, :],
        raws, cols_ref, even_ref, odd_ref, both_ref,
    )


def last_kernel(
    step_ref, u_ref, first_ref, high_ref, low_ref, raw_ref, my_cols_ref, my_even_ref, my_odd_ref, col_even_ref, col_odd_ref, row_even_ref, row_odd_ref,
    advanced_ref, tendency_ref, got_cols_ref, got_rows_ref, my_rows_ref, edge_ref, advanced_vmem, tendency_vmem, sent,
):
    half = 0.5 * step_ref[...]
    halos = unpack_borders(
        col_even_ref, col_odd_ref, row_even_ref, row_odd_ref, got_cols_ref, got_rows_ref
    )
    mine = own_borders(my_cols_ref, my_even_ref, my_odd_ref, my_rows_ref)
    copies = []

    ats = [rates(i, high_ref, low_ref, raw_ref, mine, halos, edge_ref) for i in range(2)]
    for a in range(5):
        for i in range(2):
            rows = pl.ds(8 * i, 8)
            for b in range(5):
                for v in range(4):
                    rate = final(v, b) * ats[i](v, a, b)
                    tendency_vmem[v, a, b, rows, :] = rate
                    states = u_ref[v, a, b, rows, :] + first_ref[v, a, b, rows, :]
                    advanced_vmem[v, a, b, rows, :] = 0.5 * states + half * rate
        for kept, out in ((advanced_vmem, advanced_ref), (tendency_vmem, tendency_ref)):
            copies.append(
                pltpu.make_async_copy(kept.at[:, a], out.at[:, a], sent.at[len(copies)])
            )
            copies[-1].start()
    for copy in copies:
        copy.wait()


FIELD = jax.ShapeDtypeStruct((4, 5, 5, ROWS, COLS), F32)
RAW = jax.ShapeDtypeStruct((ROWS, COLS), F32)
ROW = jax.ShapeDtypeStruct((24, COLS), F32)
WORK = jax.ShapeDtypeStruct((7, 5, 5, ROWS, COLS), F32)
TILE = jax.ShapeDtypeStruct((8, COLS), F32)
TOPS = jax.ShapeDtypeStruct((128, 1, COLS), F32)


def call(kernel, outs, scratch=(), hbm_in=False, hbm_out=False):
    here, there = pl.BlockSpec(memory_space=pltpu.VMEM), pl.BlockSpec(memory_space=pltpu.HBM)

    def run(*args):
        space = pltpu.HBM if hbm_in else pltpu.VMEM
        args = [pltpu.with_memory_space_constraint(x, space) for x in args]
        return pl.pallas_call(
            kernel,
            out_shape=tuple(o if hbm_out else pltpu.VMEM(o.shape, o.dtype) for o in outs),
            in_specs=[there if hbm_in else here for _ in args],
            out_specs=tuple(there if hbm_out else here for _ in outs),
            scratch_shapes=list(scratch),
            compiler_params=pltpu.CompilerParams(vmem_limit_bytes=16 << 20),
        )(*args)

    return run


BOTH = pltpu.VMEM((2, 24, COLS), F32)
GOT = (
    pltpu.VMEM((2, ROWS, COLS), F32),
    pltpu.VMEM((2, 24, COLS), F32),
    pltpu.VMEM((2, 24, COLS), F32),
    pltpu.VMEM((2, 32, COLS), F32),
)
FACES = pltpu.VMEM((2, 4, 5, ROWS, COLS), F32)


SWAPS = (("col_odd", 0, GX, 1), ("col_even", 0, GX, 0), ("row_odd", 2, GY, 1), ("row_even", 1, GY, 0))


def borders(cols, even, odd):
    def swap(x, axis, second):
        count = lax.axis_size(axis)
        pairs = [(i, (((i + second) ^ 1) - second) % count) for i in range(count)]
        return lax.ppermute(x, axis, pairs)

    got = {}
    for name, sent, axis, second in SWAPS:
        got[name] = swap((cols, even, odd)[sent], axis, second)
    return got["col_even"], got["col_odd"], got["row_even"], got["row_odd"]


def local(state):
    top, state = call(
        start_kernel, (TOPS, FIELD), (pltpu.SemaphoreType.DMA((5,)),), hbm_in=True
    )(state)
    tops = lax.all_to_all(top, ALL, 0, 0, tiled=True)
    raw, *mine = call(border_kernel, (RAW, RAW, ROW, ROW), (BOTH,))(state)
    halos = borders(*mine)
    work = pltpu.VMEM(WORK.shape, F32)
    high, low = call(first_volume_kernel, (FIELD, FIELD), (work, FACES))(state)
    step, first, raw, work, *next_mine = call(
        first_kernel, (TILE, FIELD, RAW, WORK, RAW, ROW, ROW), (BOTH, *GOT)
    )(tops, state, high, low, raw, *mine, *halos)
    halos = borders(*next_mine)
    high, low = call(volume_kernel, (FIELD, FIELD), (FACES,))(first, work)
    kept = pltpu.VMEM(FIELD.shape, F32)
    return call(
        last_kernel, (FIELD, FIELD), (*GOT, kept, kept, pltpu.SemaphoreType.DMA((10,))), hbm_out=True
    )(step, state, first, high, low, raw, *next_mine, *halos)


def solution(mesh):
    torus = Mesh(mesh.devices.reshape(4, 4, 4, 2), ALL)
    return jax.shard_map(
        local,
        mesh=torus,
        in_specs=(P(None, None, None, GY, GX),),
        out_specs=(P(None, None, None, GY, GX), P(None, None, None, GY, GX)),
        check_vma=False,
    )
```

profile of v0, /device:TPU:0, one launch (start us, length us, event | category | flops | bytes accessed | tf_op | source)
XLA Modules:
  0.0 35.9 jit_solution(12121624595299199266)
XLA Ops:
  0.6 2.0 %shard_map.30 = (f32[128,1,128]{2,1,0:T(1,128)}, f32[4,5,5,16,128]{4,3,2,1,0:T(8,128)S(1)}) custom-call(f32[4,5,5,16,128]{4,3,2,1,0:T(8,128)} %state_ref.1), custom_call_target="tpu_custom_call" | custom-call | tf_op jit(solution)/shard_map/pallas_call | solution.py:552
  2.6 11.2 %all-to-all-start = ((f32[128,1,128]{2,1,0:T(1,128)}), f32[128,1,128]{2,1,0:T(1,128)S(1)}, u32[]{:S(2)}, u32[]{:S(2)}) async-start(f32[128,1,128]{2,1,0:T(1,128)} %get-tuple-element.19), calls=%async_computation | async-start | bytes 131072 | tf_op jit(solution)/shard_map/all_to_all | solution.py:593
  13.8 0.3 shard_map.32
  14.1 0.0 collective-permute-start.2
  14.1 2.3 %collective-permute-start.3 = (f32[24,128]{1,0:T(8,128)S(1)}, f32[24,128]{1,0:T(8,128)S(1)}, u32[]{:S(2)}, u32[]{:S(2)}) collective-permute-start(f32[24,128]{1,0:T(8,128)S(1)} %get-tuple-element.26.my_odd_ref), channel_id=1, source_target_pairs={{0,7},{1,2},{2,1},{3,4},{4,3},{5,6},{6,5},{7,0},{8,15},{9,10},{10,... | collective-permute-start | bytes 36872 | tf_op jit(solution)/shard_map/ppermute | solution.py:581
  16.4 5.7 %collective-permute-start.1 = (f32[16,128]{1,0:T(8,128)S(1)}, f32[16,128]{1,0:T(8,128)S(1)}, u32[]{:S(2)}, u32[]{:S(2)}) collective-permute-start(f32[16,128]{1,0:T(8,128)S(1)} %get-tuple-element.24.my_cols_ref), channel_id=1, source_target_pairs={{0,120},{8,16},{16,8},{24,32},{32,24},{40,48},{48,40},{56,64},{64,... | collective-permute-start | bytes 24584 | tf_op jit(solution)/shard_map/ppermute | solution.py:581
  22.1 0.0 collective-permute-start
  22.1 2.7 %shard_map.31 = (f32[4,5,5,16,128]{4,3,2,1,0:T(8,128)S(1)}, f32[4,5,5,16,128]{4,3,2,1,0:T(8,128)S(1)}) custom-call(f32[4,5,5,16,128]{4,3,2,1,0:T(8,128)S(1)} %get-tuple-element.20.u_ref), custom_call_target="tpu_custom_call" | custom-call | tf_op jit(solution)/shard_map/pallas_call | solution.py:552
  24.8 0.0 collective-permute-done.1.col_odd_ref
  24.8 0.9 %collective-permute-done.col_even_ref = f32[16,128]{1,0:T(8,128)S(1)} collective-permute-done((f32[16,128]{1,0:T(8,128)S(1)}, f32[16,128]{1,0:T(8,128)S(1)}, u32[]{:S(2)}, u32[]{:S(2)}) %collective-permute-start) | collective-permute-done | bytes 8224 | tf_op jit(solution)/shard_map/ppermute | solution.py:581
  25.7 0.0 collective-permute-done.2.row_even_ref
  25.7 0.0 collective-permute-done.3.row_odd_ref
  25.7 0.0 all-to-all-done.tops_ref
  25.8 0.7 %shard_map.33 = (f32[8,128]{1,0:T(8,128)S(1)}, f32[4,5,5,16,128]{4,3,2,1,0:T(8,128)S(1)}, f32[16,128]{1,0:T(8,128)S(1)}, f32[7,5,5,16,128]{4,3,2,1,0:T(8,128)S(1...) custom-call(f32[128,1,128]{2,1,0:T(1,128)S(1)} %all-to-all-done.tops_ref, ...), custom_call_target="tpu_custom_call" | custom-call | tf_op jit(solution)/shard_map/pallas_call | solution.py:552
  26.4 0.0 collective-permute-start.6
  26.5 0.9 %collective-permute-start.7 = (f32[24,128]{1,0:T(8,128)S(1)}, f32[24,128]{1,0:T(8,128)S(1)}, u32[]{:S(2)}, u32[]{:S(2)}) collective-permute-start(f32[24,128]{1,0:T(8,128)S(1)} %get-tuple-element.35.my_odd_ref), channel_id=1, source_target_pairs={{0,7},{1,2},{2,1},{3,4},{4,3},{5,6},{6,5},{7,0},{8,15},{9,10},{10,... | collective-permute-start | bytes 36872 | tf_op jit(solution)/shard_map/ppermute | solution.py:581
  27.4 3.3 %collective-permute-start.5 = (f32[16,128]{1,0:T(8,128)S(1)}, f32[16,128]{1,0:T(8,128)S(1)}, u32[]{:S(2)}, u32[]{:S(2)}) collective-permute-start(f32[16,128]{1,0:T(8,128)S(1)} %get-tuple-element.33.my_cols_ref), channel_id=1, source_target_pairs={{0,120},{8,16},{16,8},{24,32},{32,24},{40,48},{48,40},{56,64},{64,... | collective-permute-start | bytes 24584 | tf_op jit(solution)/shard_map/ppermute | solution.py:581
  30.7 0.0 collective-permute-start.4
  30.7 2.6 %shard_map.34 = (f32[4,5,5,16,128]{4,3,2,1,0:T(8,128)S(1)}, f32[4,5,5,16,128]{4,3,2,1,0:T(8,128)S(1)}) custom-call(f32[4,5,5,16,128]{4,3,2,1,0:T(8,128)S(1)} %get-tuple-element.28.u_ref.first_ref, f32[7,5,5,16,128]{4,3,2,1,0:T(8,128)S(1)} %get-tuple-element.29.work_ref), custom_call_target="tpu_custom_call" | custom-call | tf_op jit(solution)/shard_map/pallas_call | solution.py:552
  33.3 1.1 %collective-permute-done.5.col_odd_ref = f32[16,128]{1,0:T(8,128)S(1)} collective-permute-done((f32[16,128]{1,0:T(8,128)S(1)}, f32[16,128]{1,0:T(8,128)S(1)}, u32[]{:S(2)}, u32[]{:S(2)}) %collective-permute-start.5) | collective-permute-done | bytes 8224 | tf_op jit(solution)/shard_map/ppermute | solution.py:581
  34.4 0.0 collective-permute-done.4.col_even_ref
  34.4 0.0 collective-permute-done.6.row_even_ref
  34.4 0.0 collective-permute-done.7.row_odd_ref
  34.4 1.6 %shard_map.35 = (f32[4,5,5,16,128]{4,3,2,1,0:T(8,128)}, f32[4,5,5,16,128]{4,3,2,1,0:T(8,128)}) custom-call(f32[8,128]{1,0:T(8,128)S(1)} %get-tuple-element.27.step_ref, f32[4,5,5,16,128]{4,3,2,1,0:T(8,128)S(1)} %get-tuple-element.20.u_ref, f32[4,5,5,16,128]{4,3,2,1,0:T(8,128)S(1)} %get-tuple-element.28.u_ref.first_ref, ...), custom_call_target="tpu_custom_call" | custom-call | tf_op jit(solution)/shard_map/pallas_call | solution.py:552
Async XLA Ops:
  2.6 23.1 %all-to-all-start = ((f32[128,1,128]{2,1,0:T(1,128)}), f32[128,1,128]{2,1,0:T(1,128)S(1)}, u32[]{:S(2)}, u32[]{:S(2)}) async-start(f32[128,1,128]{2,1,0:T(1,128)} %get-tuple-element.19), calls=%async_computation | async-start | bytes 131072 | tf_op jit(solution)/shard_map/all_to_all | solution.py:593
  14.1 11.7 %collective-permute-start.2 = (f32[24,128]{1,0:T(8,128)S(1)}, f32[24,128]{1,0:T(8,128)S(1)}, u32[]{:S(2)}, u32[]{:S(2)}) collective-permute-start(f32[24,128]{1,0:T(8,128)S(1)} %get-tuple-element.25.my_even_ref), channel_id=1, source_target_pairs={{0,1},{1,0},{2,3},{3,2},{4,5},{5,4},{6,7},{7,6},{8,9},{9,8},{10,11... | collective-permute-start | bytes 36872 | tf_op jit(solution)/shard_map/ppermute | solution.py:581
  14.1 11.6 %collective-permute-start.3 = (f32[24,128]{1,0:T(8,128)S(1)}, f32[24,128]{1,0:T(8,128)S(1)}, u32[]{:S(2)}, u32[]{:S(2)}) collective-permute-start(f32[24,128]{1,0:T(8,128)S(1)} %get-tuple-element.26.my_odd_ref), channel_id=1, source_target_pairs={{0,7},{1,2},{2,1},{3,4},{4,3},{5,6},{6,5},{7,0},{8,15},{9,10},{10,... | collective-permute-start | bytes 36872 | tf_op jit(solution)/shard_map/ppermute | solution.py:581
  16.4 8.4 %collective-permute-start.1 = (f32[16,128]{1,0:T(8,128)S(1)}, f32[16,128]{1,0:T(8,128)S(1)}, u32[]{:S(2)}, u32[]{:S(2)}) collective-permute-start(f32[16,128]{1,0:T(8,128)S(1)} %get-tuple-element.24.my_cols_ref), channel_id=1, source_target_pairs={{0,120},{8,16},{16,8},{24,32},{32,24},{40,48},{48,40},{56,64},{64,... | collective-permute-start | bytes 24584 | tf_op jit(solution)/shard_map/ppermute | solution.py:581
  22.1 3.7 %collective-permute-start = (f32[16,128]{1,0:T(8,128)S(1)}, f32[16,128]{1,0:T(8,128)S(1)}, u32[]{:S(2)}, u32[]{:S(2)}) collective-permute-start(f32[16,128]{1,0:T(8,128)S(1)} %get-tuple-element.24.my_cols_ref), channel_id=1, source_target_pairs={{0,8},{8,0},{16,24},{24,16},{32,40},{40,32},{48,56},{56,48},{64,72... | collective-permute-start | bytes 24584 | tf_op jit(solution)/shard_map/ppermute | solution.py:581
  26.4 8.0 %collective-permute-start.6 = (f32[24,128]{1,0:T(8,128)S(1)}, f32[24,128]{1,0:T(8,128)S(1)}, u32[]{:S(2)}, u32[]{:S(2)}) collective-permute-start(f32[24,128]{1,0:T(8,128)S(1)} %get-tuple-element.34.my_even_ref), channel_id=1, source_target_pairs={{0,1},{1,0},{2,3},{3,2},{4,5},{5,4},{6,7},{7,6},{8,9},{9,8},{10,11... | collective-permute-start | bytes 36872 | tf_op jit(solution)/shard_map/ppermute | solution.py:581
  26.5 7.9 %collective-permute-start.7 = (f32[24,128]{1,0:T(8,128)S(1)}, f32[24,128]{1,0:T(8,128)S(1)}, u32[]{:S(2)}, u32[]{:S(2)}) collective-permute-start(f32[24,128]{1,0:T(8,128)S(1)} %get-tuple-element.35.my_odd_ref), channel_id=1, source_target_pairs={{0,7},{1,2},{2,1},{3,4},{4,3},{5,6},{6,5},{7,0},{8,15},{9,10},{10,... | collective-permute-start | bytes 36872 | tf_op jit(solution)/shard_map/ppermute | solution.py:581
  27.4 7.0 %collective-permute-start.5 = (f32[16,128]{1,0:T(8,128)S(1)}, f32[16,128]{1,0:T(8,128)S(1)}, u32[]{:S(2)}, u32[]{:S(2)}) collective-permute-start(f32[16,128]{1,0:T(8,128)S(1)} %get-tuple-element.33.my_cols_ref), channel_id=1, source_target_pairs={{0,120},{8,16},{16,8},{24,32},{32,24},{40,48},{48,40},{56,64},{64,... | collective-permute-start | bytes 24584 | tf_op jit(solution)/shard_map/ppermute | solution.py:581
  30.7 3.7 %collective-permute-start.4 = (f32[16,128]{1,0:T(8,128)S(1)}, f32[16,128]{1,0:T(8,128)S(1)}, u32[]{:S(2)}, u32[]{:S(2)}) collective-permute-start(f32[16,128]{1,0:T(8,128)S(1)} %get-tuple-element.33.my_cols_ref), channel_id=1, source_target_pairs={{0,8},{8,0},{16,24},{24,16},{32,40},{40,32},{48,56},{56,48},{64,72... | collective-permute-start | bytes 24584 | tf_op jit(solution)/shard_map/ppermute | solution.py:581
where the time goes:
time: 36.1 us; the launch traced here: 35.9 us
  starting transfers between devices  23.5 us (65%)
  Pallas kernels  9.78 us (27%)
  waiting for transfers between devices  2 us (6%)
  between operations  0.7 us (2%)
    ppermute x8, starting transfers between devices, swap(): return lax.ppermute(x, axis, pairs)  12.3 us
    all_to_all x1, starting transfers between devices, local(): tops = lax.all_to_all(top, ALL, 0, 0, tiled=True)  11.2 us
    pallas_call x6, Pallas kernels, run(): pl.pallas_call(kernel, out_shape=tuple((o if hbm_out else pltpu.VMEM(o.sh...  9.78 us
    ppermute x8, waiting for transfers between devices, swap(): return lax.ppermute(x, axis, pairs)  2 us
  transfers between devices with their start and end apart: 9, of which 2 were waited for; matrix products, arithmetic and copies ran while one was open for 0% of the time, Pallas kernels for 15%

commit v1 on v0

--- a/solution.py
+++ b/solution.py
@@ -256,13 +256,16 @@
     return cols_ref, (rows_ref.at[1 - odd], rows_ref.at[odd])
 
 
-def start_kernel(state_ref, top_ref, u_ref, arrived):
+def start_kernel(
+    state_ref, top_ref, u_ref, raw_ref, cols_ref, even_ref, odd_ref, arrived, top_vmem, sent, both_ref
+):
     copies = [
         pltpu.make_async_copy(state_ref.at[:, a], u_ref.at[:, a], arrived.at[a]) for a in range(5)
     ]
     for copy in copies:
         copy.start()
     tops = [None, None]
+    indicators = [[[None] * 5 for _ in range(5)] for _ in range(2)]
     for a in range(5):
         copies[a].wait()
         for i in range(2):
@@ -270,29 +273,24 @@
             for b in range(5):
                 rho, mx, my, en = (u_ref[v, a, b, rows, :] for v in range(4))
                 vx, vy, p, inv_rho = velocity_pressure(rho, mx, my, en)
+                indicators[i][a][b] = rho * p
                 square = vx * vx + vy * vy
                 speed = square * lax.rsqrt(jnp.maximum(square, 1e-37))
                 square = ADIABATIC * (p * inv_rho)
                 speed = speed + square * lax.rsqrt(square)
                 tops[i] = speed if tops[i] is None else jnp.maximum(tops[i], speed)
     top = jnp.max(jnp.maximum(tops[0], tops[1]), axis=0, keepdims=True)
-    top_ref[...] = jnp.broadcast_to(top.reshape(1, 1, COLS), top_ref.shape)
-
-
-def border_kernel(u_ref, raw_ref, cols_ref, even_ref, odd_ref, both_ref):
+    top_vmem[...] = jnp.broadcast_to(top.reshape(1, 1, COLS), top_vmem.shape)
+    copy = pltpu.make_async_copy(top_vmem, top_ref, sent)
+    copy.start()
     raws = []
     for i in range(2):
-        rows = pl.ds(8 * i, 8)
-        indicator = [[None] * 5 for _ in range(5)]
-        for a in range(5):
-            for b in range(5):
-                cons = [u_ref[v, a, b, rows, :] for v in range(4)]
-                indicator[a][b] = cons[0] * velocity_pressure(*cons)[2]
-        raws.append(raw_indicator(indicator))
-        raw_ref[rows, :] = raws[i]
+        raws.append(raw_indicator(indicators[i]))
+        raw_ref[pl.ds(8 * i, 8), :] = raws[i]
     pack_borders(
         lambda v, a, b, rows: u_ref[v, a, b, rows, :], raws, cols_ref, even_ref, odd_ref, both_ref
     )
+    copy.wait()
 
 
 ORDER = ((0, 1, 2, 3), (0, 2, 1, 3))
@@ -470,29 +468,38 @@
     return (COURANT * 2.0 / 9.0) / jnp.broadcast_to(top, (8, COLS))
 
 
+def rate_kernel(
+    high_ref, low_ref, raw_ref, my_cols_ref, my_even_ref, my_odd_ref, col_even_ref, col_odd_ref, row_even_ref, row_odd_ref,
+    rate_ref, got_cols_ref, got_rows_ref, my_rows_ref, edge_ref,
+):
+    halos = unpack_borders(
+        col_even_ref, col_odd_ref, row_even_ref, row_odd_ref, got_cols_ref, got_rows_ref
+    )
+    mine = own_borders(my_cols_ref, my_even_ref, my_odd_ref, my_rows_ref)
+    for i in range(2):
+        at = rates(i, high_ref, low_ref, raw_ref, mine, halos, edge_ref)
+        for a, b, v in NODES:
+            rate_ref[v, a, b, pl.ds(8 * i, 8), :] = at(v, a, b)
+
+
 def first_kernel(
-    tops_ref, u_ref, high_ref, low_ref, raw_ref, my_cols_ref, my_even_ref, my_odd_ref, col_even_ref, col_odd_ref, row_even_ref, row_odd_ref,
-    step_ref, first_ref, next_raw_ref, next_work_ref, cols_ref, even_ref, odd_ref, both_ref, got_cols_ref, got_rows_ref, my_rows_ref, edge_ref,
+    tops_ref, u_ref, rate_ref,
+    step_ref, first_ref, next_raw_ref, next_work_ref, cols_ref, even_ref, odd_ref, both_ref,
 ):
     step = step_of(tops_ref)
     step_ref[...] = step
     steps = {(v, b): final(v, b) * step for v in (0, 1) for b in range(5)}
-    halos = unpack_borders(
-        col_even_ref, col_odd_ref, row_even_ref, row_odd_ref, got_cols_ref, got_rows_ref
-    )
-
-    mine = own_borders(my_cols_ref, my_even_ref, my_odd_ref, my_rows_ref)
-
     raws = []
     for i in range(2):
         rows = pl.ds(8 * i, 8)
-        at = rates(i, high_ref, low_ref, raw_ref, mine, halos, edge_ref)
-        for a, b, v in NODES:
-            first_ref[v, a, b, rows, :] = u_ref[v, a, b, rows, :] + steps[min(v, 1), b] * at(v, a, b)
         indicator = [[None] * 5 for _ in range(5)]
         for a in range(5):
             for b in range(5):
-                cons = [first_ref[v, a, b, rows, :] for v in range(4)]
+                cons = []
+                for v in range(4):
+                    change = steps[min(v, 1), b] * rate_ref[v, a, b, rows, :]
+                    cons.append(u_ref[v, a, b, rows, :] + change)
+                    first_ref[v, a, b, rows, :] = cons[v]
                 values = derived(*cons)
                 for k, x in enumerate(values):
                     next_work_ref[k, a, b, rows, :] = x
@@ -543,7 +550,7 @@
 TOPS = jax.ShapeDtypeStruct((128, 1, COLS), F32)
 
 
-def call(kernel, outs, scratch=(), hbm_in=False, hbm_out=False):
+def call(kernel, outs, scratch=(), hbm_in=False, hbm_out=0):
     here, there = pl.BlockSpec(memory_space=pltpu.VMEM), pl.BlockSpec(memory_space=pltpu.HBM)
 
     def run(*args):
@@ -551,9 +558,11 @@
         args = [pltpu.with_memory_space_constraint(x, space) for x in args]
         return pl.pallas_call(
             kernel,
-            out_shape=tuple(o if hbm_out else pltpu.VMEM(o.shape, o.dtype) for o in outs),
+            out_shape=tuple(
+                o if k < hbm_out else pltpu.VMEM(o.shape, o.dtype) for k, o in enumerate(outs)
+            ),
             in_specs=[there if hbm_in else here for _ in args],
-            out_specs=tuple(there if hbm_out else here for _ in outs),
+            out_specs=tuple(there if k < hbm_out else here for k, _ in enumerate(outs)),
             scratch_shapes=list(scratch),
             compiler_params=pltpu.CompilerParams(vmem_limit_bytes=16 << 20),
         )(*args)
@@ -587,22 +596,28 @@
 
 
 def local(state):
-    top, state = call(
-        start_kernel, (TOPS, FIELD), (pltpu.SemaphoreType.DMA((5,)),), hbm_in=True
+    scratch = (
+        pltpu.SemaphoreType.DMA((5,)),
+        pltpu.VMEM(TOPS.shape, F32),
+        pltpu.SemaphoreType.DMA,
+        BOTH,
+    )
+    top, state, raw, *mine = call(
+        start_kernel, (TOPS, FIELD, RAW, RAW, ROW, ROW), scratch, hbm_in=True, hbm_out=1
     )(state)
+    work = pltpu.VMEM(WORK.shape, F32)
     tops = lax.all_to_all(top, ALL, 0, 0, tiled=True)
-    raw, *mine = call(border_kernel, (RAW, RAW, ROW, ROW), (BOTH,))(state)
     halos = borders(*mine)
-    work = pltpu.VMEM(WORK.shape, F32)
     high, low = call(first_volume_kernel, (FIELD, FIELD), (work, FACES))(state)
+    (rate,) = call(rate_kernel, (FIELD,), GOT)(high, low, raw, *mine, *halos)
     step, first, raw, work, *next_mine = call(
-        first_kernel, (TILE, FIELD, RAW, WORK, RAW, ROW, ROW), (BOTH, *GOT)
-    )(tops, state, high, low, raw, *mine, *halos)
+        first_kernel, (TILE, FIELD, RAW, WORK, RAW, ROW, ROW), (BOTH,)
+    )(tops, state, rate)
     halos = borders(*next_mine)
     high, low = call(volume_kernel, (FIELD, FIELD), (FACES,))(first, work)
     kept = pltpu.VMEM(FIELD.shape, F32)
     return call(
-        last_kernel, (FIELD, FIELD), (*GOT, kept, kept, pltpu.SemaphoreType.DMA((10,))), hbm_out=True
+        last_kernel, (FIELD, FIELD), (*GOT, kept, kept, pltpu.SemaphoreType.DMA((10,))), hbm_out=2
     )(step, state, first, high, low, raw, *next_mine, *halos)
 
 

time: 36.1 us -> 36.2 us (level)
  transfers between devices with their start and end apart: 9 -> 9, of which waited for: 2 -> 2; matrix products, arithmetic and copies ran while one was open for 0% -> 0% of each run, Pallas kernels for 15% -> 16%
where the time goes in v1:
time: 36.2 us; the launch traced here: 36 us
  starting transfers between devices  23.5 us (65%)
  Pallas kernels  9.79 us (27%)
  waiting for transfers between devices  1.99 us (5%)
  between operations  0.7 us (2%)
    ppermute x8, starting transfers between devices, swap(): return lax.ppermute(x, axis, pairs)  12.4 us
    all_to_all x1, starting transfers between devices, local(): tops = lax.all_to_all(top, ALL, 0, 0, tiled=True)  11.2 us
    pallas_call x6, Pallas kernels, run(): pl.pallas_call(kernel, out_shape=tuple((o if k < hbm_out else pltpu.VMEM(...  9.79 us
    ppermute x8, waiting for transfers between devices, swap(): return lax.ppermute(x, axis, pairs)  1.98 us
  transfers between devices with their start and end apart: 9, of which 2 were waited for; matrix products, arithmetic and copies ran while one was open for 0% of the time, Pallas kernels for 16%

profile of v1, /device:TPU:0, one launch (start us, length us, event | category | flops | bytes accessed | tf_op | source)
XLA Modules:
  0.0 36.0 jit_solution(5886806853039484035)
XLA Ops:
  0.6 2.1 %shard_map.30 = (f32[128,1,128]{2,1,0:T(1,128)}, f32[4,5,5,16,128]{4,3,2,1,0:T(8,128)S(1)}, f32[16,128]{1,0:T(8,128)S(1)}, f32[16,128]{1,0:T(8,128)S(1)}, f32[24,128]{1,0:T(8,128)S(1)}, /*index=5*/f32[24,128]{1,0:T(8,128)S(1)}) custom-call(f32[4,5,5,16,128]{4,3,2,1,0:T(8,128)} %state_ref.1), custom_call_target="tpu_custom_call" | custom-call | tf_op jit(solution)/shard_map/pallas_call | solution.py:559
  2.7 11.2 %all-to-all-start = ((f32[128,1,128]{2,1,0:T(1,128)}), f32[128,1,128]{2,1,0:T(1,128)S(1)}, u32[]{:S(2)}, u32[]{:S(2)}) async-start(f32[128,1,128]{2,1,0:T(1,128)} %get-tuple-element.19), calls=%async_computation | async-start | bytes 131072 | tf_op jit(solution)/shard_map/all_to_all | solution.py:609
  13.9 0.1 collective-permute-start.2
  14.0 2.3 %collective-permute-start.3 = (f32[24,128]{1,0:T(8,128)S(1)}, f32[24,128]{1,0:T(8,128)S(1)}, u32[]{:S(2)}, u32[]{:S(2)}) collective-permute-start(f32[24,128]{1,0:T(8,128)S(1)} %get-tuple-element.26.my_odd_ref), channel_id=1, source_target_pairs={{0,7},{1,2},{2,1},{3,4},{4,3},{5,6},{6,5},{7,0},{8,15},{9,10},{10,... | collective-permute-start | bytes 36872 | tf_op jit(solution)/shard_map/ppermute | solution.py:590
  16.3 5.7 %collective-permute-start.1 = (f32[16,128]{1,0:T(8,128)S(1)}, f32[16,128]{1,0:T(8,128)S(1)}, u32[]{:S(2)}, u32[]{:S(2)}) collective-permute-start(f32[16,128]{1,0:T(8,128)S(1)} %get-tuple-element.24.my_cols_ref), channel_id=1, source_target_pairs={{0,120},{8,16},{16,8},{24,32},{32,24},{40,48},{48,40},{56,64},{64,... | collective-permute-start | bytes 24584 | tf_op jit(solution)/shard_map/ppermute | solution.py:590
  22.0 0.0 collective-permute-start
  22.0 2.7 %shard_map.31 = (f32[4,5,5,16,128]{4,3,2,1,0:T(8,128)S(1)}, f32[4,5,5,16,128]{4,3,2,1,0:T(8,128)S(1)}) custom-call(f32[4,5,5,16,128]{4,3,2,1,0:T(8,128)S(1)} %get-tuple-element.20.u_ref), custom_call_target="tpu_custom_call" | custom-call | tf_op jit(solution)/shard_map/pallas_call | solution.py:559
  24.7 0.0 collective-permute-done.1.col_odd_ref
  24.7 0.9 %collective-permute-done.col_even_ref = f32[16,128]{1,0:T(8,128)S(1)} collective-permute-done((f32[16,128]{1,0:T(8,128)S(1)}, f32[16,128]{1,0:T(8,128)S(1)}, u32[]{:S(2)}, u32[]{:S(2)}) %collective-permute-start) | collective-permute-done | bytes 8224 | tf_op jit(solution)/shard_map/ppermute | solution.py:590
  25.6 0.0 collective-permute-done.2.row_even_ref
  25.6 0.0 collective-permute-done.3.row_odd_ref
  25.6 0.3 shard_map.32.rate_ref
  25.9 0.0 all-to-all-done.tops_ref
  25.9 0.5 %shard_map.33 = (f32[8,128]{1,0:T(8,128)S(1)}, f32[4,5,5,16,128]{4,3,2,1,0:T(8,128)S(1)}, f32[16,128]{1,0:T(8,128)S(1)}, f32[7,5,5,16,128]{4,3,2,1,0:T(8,128)S(1...) custom-call(f32[128,1,128]{2,1,0:T(1,128)S(1)} %all-to-all-done.tops_ref, ...), custom_call_target="tpu_custom_call" | custom-call | tf_op jit(solution)/shard_map/pallas_call | solution.py:559
  26.5 0.0 collective-permute-start.6
  26.5 0.9 %collective-permute-start.7 = (f32[24,128]{1,0:T(8,128)S(1)}, f32[24,128]{1,0:T(8,128)S(1)}, u32[]{:S(2)}, u32[]{:S(2)}) collective-permute-start(f32[24,128]{1,0:T(8,128)S(1)} %get-tuple-element.35.my_odd_ref), channel_id=1, source_target_pairs={{0,7},{1,2},{2,1},{3,4},{4,3},{5,6},{6,5},{7,0},{8,15},{9,10},{10,... | collective-permute-start | bytes 36872 | tf_op jit(solution)/shard_map/ppermute | solution.py:590
  27.4 3.3 %collective-permute-start.5 = (f32[16,128]{1,0:T(8,128)S(1)}, f32[16,128]{1,0:T(8,128)S(1)}, u32[]{:S(2)}, u32[]{:S(2)}) collective-permute-start(f32[16,128]{1,0:T(8,128)S(1)} %get-tuple-element.33.my_cols_ref), channel_id=1, source_target_pairs={{0,120},{8,16},{16,8},{24,32},{32,24},{40,48},{48,40},{56,64},{64,... | collective-permute-start | bytes 24584 | tf_op jit(solution)/shard_map/ppermute | solution.py:590
  30.8 0.0 collective-permute-start.4
  30.8 2.6 %shard_map.34 = (f32[4,5,5,16,128]{4,3,2,1,0:T(8,128)S(1)}, f32[4,5,5,16,128]{4,3,2,1,0:T(8,128)S(1)}) custom-call(f32[4,5,5,16,128]{4,3,2,1,0:T(8,128)S(1)} %get-tuple-element.28.u_ref.first_ref, f32[7,5,5,16,128]{4,3,2,1,0:T(8,128)S(1)} %get-tuple-element.29.work_ref), custom_call_target="tpu_custom_call" | custom-call | tf_op jit(solution)/shard_map/pallas_call | solution.py:559
  33.4 1.0 %collective-permute-done.5.col_odd_ref = f32[16,128]{1,0:T(8,128)S(1)} collective-permute-done((f32[16,128]{1,0:T(8,128)S(1)}, f32[16,128]{1,0:T(8,128)S(1)}, u32[]{:S(2)}, u32[]{:S(2)}) %collective-permute-start.5) | collective-permute-done | bytes 8224 | tf_op jit(solution)/shard_map/ppermute | solution.py:590
  34.4 0.0 collective-permute-done.4.col_even_ref
  34.4 0.0 collective-permute-done.6.row_even_ref
  34.4 0.0 collective-permute-done.7.row_odd_ref
  34.4 1.6 %shard_map.35 = (f32[4,5,5,16,128]{4,3,2,1,0:T(8,128)}, f32[4,5,5,16,128]{4,3,2,1,0:T(8,128)}) custom-call(f32[8,128]{1,0:T(8,128)S(1)} %get-tuple-element.27.step_ref, f32[4,5,5,16,128]{4,3,2,1,0:T(8,128)S(1)} %get-tuple-element.20.u_ref, f32[4,5,5,16,128]{4,3,2,1,0:T(8,128)S(1)} %get-tuple-element.28.u_ref.first_ref, ...), custom_call_target="tpu_custom_call" | custom-call | tf_op jit(solution)/shard_map/pallas_call | solution.py:559
Async XLA Ops:
  2.7 23.2 %all-to-all-start = ((f32[128,1,128]{2,1,0:T(1,128)}), f32[128,1,128]{2,1,0:T(1,128)S(1)}, u32[]{:S(2)}, u32[]{:S(2)}) async-start(f32[128,1,128]{2,1,0:T(1,128)} %get-tuple-element.19), calls=%async_computation | async-start | bytes 131072 | tf_op jit(solution)/shard_map/all_to_all | solution.py:609
  13.9 11.7 %collective-permute-start.2 = (f32[24,128]{1,0:T(8,128)S(1)}, f32[24,128]{1,0:T(8,128)S(1)}, u32[]{:S(2)}, u32[]{:S(2)}) collective-permute-start(f32[24,128]{1,0:T(8,128)S(1)} %get-tuple-element.25.my_even_ref), channel_id=1, source_target_pairs={{0,1},{1,0},{2,3},{3,2},{4,5},{5,4},{6,7},{7,6},{8,9},{9,8},{10,11... | collective-permute-start | bytes 36872 | tf_op jit(solution)/shard_map/ppermute | solution.py:590
  14.0 11.6 %collective-permute-start.3 = (f32[24,128]{1,0:T(8,128)S(1)}, f32[24,128]{1,0:T(8,128)S(1)}, u32[]{:S(2)}, u32[]{:S(2)}) collective-permute-start(f32[24,128]{1,0:T(8,128)S(1)} %get-tuple-element.26.my_odd_ref), channel_id=1, source_target_pairs={{0,7},{1,2},{2,1},{3,4},{4,3},{5,6},{6,5},{7,0},{8,15},{9,10},{10,... | collective-permute-start | bytes 36872 | tf_op jit(solution)/shard_map/ppermute | solution.py:590
  16.3 8.4 %collective-permute-start.1 = (f32[16,128]{1,0:T(8,128)S(1)}, f32[16,128]{1,0:T(8,128)S(1)}, u32[]{:S(2)}, u32[]{:S(2)}) collective-permute-start(f32[16,128]{1,0:T(8,128)S(1)} %get-tuple-element.24.my_cols_ref), channel_id=1, source_target_pairs={{0,120},{8,16},{16,8},{24,32},{32,24},{40,48},{48,40},{56,64},{64,... | collective-permute-start | bytes 24584 | tf_op jit(solution)/shard_map/ppermute | solution.py:590
  22.0 3.7 %collective-permute-start = (f32[16,128]{1,0:T(8,128)S(1)}, f32[16,128]{1,0:T(8,128)S(1)}, u32[]{:S(2)}, u32[]{:S(2)}) collective-permute-start(f32[16,128]{1,0:T(8,128)S(1)} %get-tuple-element.24.my_cols_ref), channel_id=1, source_target_pairs={{0,8},{8,0},{16,24},{24,16},{32,40},{40,32},{48,56},{56,48},{64,72... | collective-permute-start | bytes 24584 | tf_op jit(solution)/shard_map/ppermute | solution.py:590
  26.5 8.0 %collective-permute-start.6 = (f32[24,128]{1,0:T(8,128)S(1)}, f32[24,128]{1,0:T(8,128)S(1)}, u32[]{:S(2)}, u32[]{:S(2)}) collective-permute-start(f32[24,128]{1,0:T(8,128)S(1)} %get-tuple-element.34.my_even_ref), channel_id=1, source_target_pairs={{0,1},{1,0},{2,3},{3,2},{4,5},{5,4},{6,7},{7,6},{8,9},{9,8},{10,11... | collective-permute-start | bytes 36872 | tf_op jit(solution)/shard_map/ppermute | solution.py:590
  26.5 7.9 %collective-permute-start.7 = (f32[24,128]{1,0:T(8,128)S(1)}, f32[24,128]{1,0:T(8,128)S(1)}, u32[]{:S(2)}, u32[]{:S(2)}) collective-permute-start(f32[24,128]{1,0:T(8,128)S(1)} %get-tuple-element.35.my_odd_ref), channel_id=1, source_target_pairs={{0,7},{1,2},{2,1},{3,4},{4,3},{5,6},{6,5},{7,0},{8,15},{9,10},{10,... | collective-permute-start | bytes 36872 | tf_op jit(solution)/shard_map/ppermute | solution.py:590
  27.4 7.0 %collective-permute-start.5 = (f32[16,128]{1,0:T(8,128)S(1)}, f32[16,128]{1,0:T(8,128)S(1)}, u32[]{:S(2)}, u32[]{:S(2)}) collective-permute-start(f32[16,128]{1,0:T(8,128)S(1)} %get-tuple-element.33.my_cols_ref), channel_id=1, source_target_pairs={{0,120},{8,16},{16,8},{24,32},{32,24},{40,48},{48,40},{56,64},{64,... | collective-permute-start | bytes 24584 | tf_op jit(solution)/shard_map/ppermute | solution.py:590
  30.8 3.7 %collective-permute-start.4 = (f32[16,128]{1,0:T(8,128)S(1)}, f32[16,128]{1,0:T(8,128)S(1)}, u32[]{:S(2)}, u32[]{:S(2)}) collective-permute-start(f32[16,128]{1,0:T(8,128)S(1)} %get-tuple-element.33.my_cols_ref), channel_id=1, source_target_pairs={{0,8},{8,0},{16,24},{24,16},{32,40},{40,32},{48,56},{56,48},{64,72... | collective-permute-start | bytes 24584 | tf_op jit(solution)/shard_map/ppermute | solution.py:590
